TPU v7x, 32 devices: a whole 2x2x4 slice. The times are simulated.
32 devices in a mesh: dp: 8 (over y, x, core), tensor: 4 (over z).
Axes of the slice: x: 2, y: 2, z: 4, core: 2. Of those that a mesh axis runs over, the one named last changes fastest.
Arguments:
- hidden_in: float32 [8192, 2048], P(('dp', 'tensor')), may hold values from -6 to 6
- positions: int32 [8192], P('dp'), may hold values from 0 to 4095
- norm_gains: bfloat16 [1, 2, 2048], P(None, None, ('dp', 'tensor')), may hold values from 0.25 to 1.75
- w_query: bfloat16 [1, 2048, 2048], P(None, 'dp', 'tensor'), may hold values from -0.125 to 0.125
- w_key: bfloat16 [1, 2048, 256], P(None, ('dp', 'tensor')), may hold values from -0.125 to 0.125
- w_value: bfloat16 [1, 2048, 256], P(None, ('dp', 'tensor')), may hold values from -0.125 to 0.125
- w_out: bfloat16 [1, 2048, 2048], P(None, 'tensor', 'dp'), may hold values from -0.5 to 0.5
- w_gate: bfloat16 [1, 2048, 5632], P(None, 'dp', 'tensor'), may hold values from -0.125 to 0.125
- w_up: bfloat16 [1, 2048, 5632], P(None, 'dp', 'tensor'), may hold values from -0.125 to 0.125
- w_down: bfloat16 [1, 5632, 2048], P(None, 'tensor', 'dp'), may hold values from -0.078125 to 0.078125
- out_grad: float32 [8192, 2048], P(('dp', 'tensor')), may hold values from -6 to 6
Outputs:
- hidden_out: float32 [8192, 2048], P(('dp', 'tensor'))
- grad_in: float32 [8192, 2048], P(('dp', 'tensor'))
- grad_gains: float32 [1, 2, 2048], P(None, None, ('dp', 'tensor'))
- grad_query: float32 [1, 2048, 2048], P(None, 'dp', 'tensor')
- grad_key: float32 [1, 2048, 256], P(None, ('dp', 'tensor'))
- grad_value: float32 [1, 2048, 256], P(None, ('dp', 'tensor'))
- grad_out: float32 [1, 2048, 2048], P(None, 'tensor', 'dp')
- grad_gate: float32 [1, 2048, 5632], P(None, 'dp', 'tensor')
- grad_up: float32 [1, 2048, 5632], P(None, 'dp', 'tensor')
- grad_down: float32 [1, 5632, 2048], P(None, 'tensor', 'dp')
All inputs are finite; a program needn't handle non-finite values.
Results may differ from a plain program's by a relative error of at most 0.019.
Values may be sent and summed in bfloat16 or wider, within the bound.
A program may use at most 192 MiB of HBM per device.

v0:
```python
import jax
import jax.numpy as jnp
from jax import lax
from jax.sharding import PartitionSpec as P

D = 2048
H = 32
KV = 4
HD = 64
SEQ = 128
NORM_EPS = 1e-05
NEG_BIG = -1e30


def rms_normed(row_vals, gain_vec):
    inv_rms = lax.rsqrt(jnp.mean(row_vals * row_vals, -1, keepdims=True) + NORM_EPS)
    return (row_vals * inv_rms * gain_vec.astype(jnp.float32)).astype(jnp.bfloat16)


def rms_back(row_vals, gain_vec, grad_normed):
    inv_rms = lax.rsqrt(jnp.mean(row_vals * row_vals, -1, keepdims=True) + NORM_EPS)
    weighted = grad_normed * gain_vec.astype(jnp.float32)
    grad_gain = jnp.sum(grad_normed * row_vals * inv_rms, 0)
    grad_rows = inv_rms * weighted - row_vals * inv_rms**3 * jnp.mean(
        weighted * row_vals, -1, keepdims=True
    )
    return (grad_rows, grad_gain)


def rope_tables(positions):
    inv_freq = 10000.0 ** (-(jnp.arange(HD // 2, dtype=jnp.float32) * 2.0 / HD))
    angles = positions.astype(jnp.float32)[:, None] * inv_freq[None, :]
    return (jnp.cos(angles), jnp.sin(angles))


def rotate(row_vals, cosine_tab, sine_tab):
    row_total = row_vals.shape[0]
    shaped = row_vals.reshape(row_total, -1, HD)
    front_half = shaped[..., : HD // 2]
    back_half = shaped[..., HD // 2 :]
    cos_part = cosine_tab[:, None, :]
    sin_part = sine_tab[:, None, :]
    turned = jnp.concatenate(
        [
            front_half * cos_part - back_half * sin_part,
            back_half * cos_part + front_half * sin_part,
        ],
        -1,
    )
    return turned.reshape(row_total, -1)


def rotate_back(row_vals, cosine_tab, sine_tab):
    row_total = row_vals.shape[0]
    shaped = row_vals.reshape(row_total, -1, HD)
    front_half = shaped[..., : HD // 2]
    back_half = shaped[..., HD // 2 :]
    cos_part = cosine_tab[:, None, :]
    sin_part = sine_tab[:, None, :]
    turned = jnp.concatenate(
        [
            front_half * cos_part + back_half * sin_part,
            back_half * cos_part - front_half * sin_part,
        ],
        -1,
    )
    return turned.reshape(row_total, -1)


def head_major(values_in, seq_len):
    head_count = values_in.shape[1] // HD
    return (
        values_in.reshape(seq_len, head_count, HD)
        .transpose(1, 0, 2)
        .reshape(head_count * seq_len, HD)
    )


def seq_major(values_in, seq_len):
    head_count = values_in.shape[0] // seq_len
    return (
        values_in.reshape(head_count, seq_len, HD)
        .transpose(1, 0, 2)
        .reshape(seq_len, head_count * HD)
    )


def causal_scores(query_rows, key_rows):
    seq_len = key_rows.shape[0]
    scores = jnp.dot(query_rows, key_rows.T, preferred_element_type=jnp.float32) * HD ** (-0.5)
    row_pos = lax.broadcasted_iota(jnp.int32, scores.shape, 0) % seq_len
    col_pos = lax.broadcasted_iota(jnp.int32, scores.shape, 1)
    return jnp.where(col_pos <= row_pos, scores, NEG_BIG)


def attend_forward(query_rows, key_rows, value_rows):
    scores = causal_scores(query_rows, key_rows)
    row_max = jnp.max(scores, -1, keepdims=True)
    log_total = row_max[:, 0] + jnp.log(jnp.sum(jnp.exp(scores - row_max), -1))
    attn_prob = jnp.exp(scores - log_total[:, None]).astype(jnp.bfloat16)
    return (jnp.dot(attn_prob, value_rows, preferred_element_type=jnp.float32), log_total)


def attend_backward(query_rows, key_rows, value_rows, log_total, grad_rows):
    seq_len = key_rows.shape[0]
    head_count = query_rows.shape[0] // seq_len
    scores = causal_scores(query_rows, key_rows)
    attn_prob = jnp.exp(scores - log_total[:, None])
    prob_bf = attn_prob.astype(jnp.bfloat16)
    grad_prob = jnp.dot(grad_rows, value_rows.T, preferred_element_type=jnp.float32)
    delta = jnp.sum(attn_prob * grad_prob, -1, keepdims=True)
    grad_scores = (attn_prob * (grad_prob - delta) * HD ** (-0.5)).astype(jnp.bfloat16)
    grad_query = jnp.dot(grad_scores, key_rows, preferred_element_type=jnp.float32)
    scores_3d = grad_scores.reshape(head_count, seq_len, seq_len)
    query_3d = query_rows.reshape(head_count, seq_len, HD)
    prob_3d = prob_bf.reshape(head_count, seq_len, seq_len)
    grad_3d = grad_rows.reshape(head_count, seq_len, HD)
    grad_key = jnp.einsum("hqk,hqd->hkd", scores_3d, query_3d, preferred_element_type=jnp.float32)
    grad_value = jnp.einsum("hqk,hqd->hkd", prob_3d, grad_3d, preferred_element_type=jnp.float32)
    return (
        grad_query,
        grad_key.reshape(head_count * seq_len, HD),
        grad_value.reshape(head_count * seq_len, HD),
    )


def tdot(left_op, right_op):
    return lax.dot_general(
        left_op, right_op, (((0,), (0,)), ((), ())), preferred_element_type=jnp.float32
    )


def fetch_weights(layer_index, w_query, w_key, w_value, w_out, w_gate, w_up, w_down, norm_gains):
    large = (
        lax.all_gather(w_query[layer_index], "dp", axis=0, tiled=True),
        lax.all_gather(w_out[layer_index], "dp", axis=1, tiled=True),
        lax.all_gather(w_gate[layer_index], "dp", axis=0, tiled=True),
        lax.all_gather(w_up[layer_index], "dp", axis=0, tiled=True),
        lax.all_gather(w_down[layer_index], "dp", axis=1, tiled=True),
    )
    small = (
        lax.all_gather(w_key[layer_index], ("dp", "tensor"), axis=0, tiled=True),
        lax.all_gather(w_value[layer_index], ("dp", "tensor"), axis=0, tiled=True),
        lax.all_gather(norm_gains[layer_index], ("dp", "tensor"), axis=1, tiled=True),
    )
    return tuple(large) + tuple(small)


def gather_rows(row_vals):
    return lax.all_gather(row_vals, "tensor", axis=0, tiled=True)


def sum_rows(term, rows_dev):
    return lax.psum_scatter(
        term(jnp.int32(0), rows_dev * lax.axis_size("tensor")),
        "tensor",
        scatter_dimension=0,
        tiled=True,
    )


def on_device(
    hidden_in, positions, norm_gains, w_query, w_key, w_value, w_out, w_gate, w_up, w_down, out_grad
):
    rows_dev = hidden_in.shape[0]
    block_rows = positions.shape[0]
    seq_count = block_rows // SEQ
    layers = w_query.shape[0]
    heads_dev = w_query.shape[2] // HD
    kv_head = lax.axis_index("tensor") * heads_dev // (H // KV)
    cosine_tab, sine_tab = rope_tables(positions)

    def pick_head(weight_kv):
        return lax.dynamic_slice_in_dim(weight_kv, kv_head * HD, HD, 1)

    def by_sequence(values_in):
        return values_in.reshape(seq_count, SEQ, -1)

    def one_forward(pieces):
        query_seq, key_seq, value_seq = pieces
        attended, log_total = attend_forward(head_major(query_seq, SEQ), key_seq, value_seq)
        return (seq_major(attended, SEQ).astype(jnp.bfloat16), log_total)

    def one_backward(pieces):
        query_seq, key_seq, value_seq, log_seq, grad_seq = pieces
        grad_query, grad_key, grad_value = attend_backward(
            head_major(query_seq, SEQ), key_seq, value_seq, log_seq, head_major(grad_seq, SEQ)
        )
        return (seq_major(grad_query, SEQ), seq_major(grad_key, SEQ), seq_major(grad_value, SEQ))

    layer_index = 0
    weights = fetch_weights(
        layer_index, w_query, w_key, w_value, w_out, w_gate, w_up, w_down, norm_gains
    )
    wq, wo, wg, wu, wd, wk_all, wv_all, gain_pair = weights
    wk = pick_head(wk_all)
    wv = pick_head(wv_all)
    normed_one = gather_rows(rms_normed(hidden_in, gain_pair[0]))
    query_all = rotate(
        jnp.dot(normed_one, wq, preferred_element_type=jnp.float32), cosine_tab, sine_tab
    ).astype(jnp.bfloat16)
    key_all = rotate(
        jnp.dot(normed_one, wk, preferred_element_type=jnp.float32), cosine_tab, sine_tab
    ).astype(jnp.bfloat16)
    value_all = jnp.dot(normed_one, wv, preferred_element_type=jnp.float32).astype(jnp.bfloat16)
    attended, log_total = lax.map(
        one_forward, (by_sequence(query_all), by_sequence(key_all), by_sequence(value_all))
    )
    attended = attended.reshape(block_rows, -1)
    middle = hidden_in + sum_rows(
        lambda offset, length: jnp.dot(attended, wo, preferred_element_type=jnp.float32), rows_dev
    )
    normed_two = gather_rows(rms_normed(middle, gain_pair[1]))
    gate_pre = jnp.dot(normed_two, wg, preferred_element_type=jnp.float32)
    up_pre = jnp.dot(normed_two, wu, preferred_element_type=jnp.float32)
    hidden = (gate_pre * jax.nn.sigmoid(gate_pre) * up_pre).astype(jnp.bfloat16)
    output = middle + sum_rows(
        lambda offset, length: jnp.dot(hidden, wd, preferred_element_type=jnp.float32), rows_dev
    )
    saved = [
        (
            hidden_in,
            normed_one,
            query_all,
            key_all,
            value_all,
            attended,
            log_total,
            middle,
            normed_two,
            gate_pre,
            up_pre,
            hidden,
        )
    ]
    cotangent = out_grad
    layer_grads = [None] * layers
    for layer_index in reversed(range(layers)):
        weights = fetch_weights(
            layer_index, w_query, w_key, w_value, w_out, w_gate, w_up, w_down, norm_gains
        )
        wq, wo, wg, wu, wd, wk_all, wv_all, gain_pair = weights
        wk = pick_head(wk_all)
        wv = pick_head(wv_all)
        (
            layer_in,
            normed_one,
            query_all,
            key_all,
            value_all,
            attended,
            log_total,
            middle,
            normed_two,
            gate_pre,
            up_pre,
            hidden,
        ) = saved[layer_index]
        top_all = gather_rows(cotangent.astype(jnp.bfloat16))
        grad_down = tdot(hidden, top_all)
        grad_hidden = jnp.dot(top_all, wd.T, preferred_element_type=jnp.float32)
        sigmoid_gate = jax.nn.sigmoid(gate_pre)
        grad_gate_pre = (
            grad_hidden * up_pre * sigmoid_gate * (1.0 + gate_pre * (1.0 - sigmoid_gate))
        ).astype(jnp.bfloat16)
        grad_up_pre = (grad_hidden * gate_pre * sigmoid_gate).astype(jnp.bfloat16)
        grad_gate = tdot(normed_two, grad_gate_pre)
        grad_up = tdot(normed_two, grad_up_pre)
        grad_normed_two = sum_rows(
            lambda offset, length: jnp.dot(grad_gate_pre, wg.T, preferred_element_type=jnp.float32)
            + jnp.dot(grad_up_pre, wu.T, preferred_element_type=jnp.float32),
            rows_dev,
        )
        grad_mid_norm, grad_gain_two = rms_back(middle, gain_pair[1], grad_normed_two)
        grad_middle = cotangent + grad_mid_norm
        middle_all = gather_rows(grad_middle.astype(jnp.bfloat16))
        grad_out = tdot(attended, middle_all)
        grad_attended = jnp.dot(middle_all, wo.T, preferred_element_type=jnp.float32).astype(
            jnp.bfloat16
        )
        grads = lax.map(
            one_backward,
            (
                by_sequence(query_all),
                by_sequence(key_all),
                by_sequence(value_all),
                log_total,
                by_sequence(grad_attended),
            ),
        )
        grad_q = rotate_back(grads[0].reshape(block_rows, -1), cosine_tab, sine_tab).astype(
            jnp.bfloat16
        )
        grad_k = rotate_back(grads[1].reshape(block_rows, -1), cosine_tab, sine_tab).astype(
            jnp.bfloat16
        )
        grad_v = grads[2].reshape(block_rows, -1).astype(jnp.bfloat16)
        grad_query = tdot(normed_one, grad_q)
        key_local = jnp.sum(tdot(normed_one, grad_k).reshape(D, heads_dev, HD), 1)
        value_local = jnp.sum(tdot(normed_one, grad_v).reshape(D, heads_dev, HD), 1)
        wk_tiled = jnp.tile(wk, (1, heads_dev))
        wv_tiled = jnp.tile(wv, (1, heads_dev))
        grad_normed_one = sum_rows(
            lambda offset, length: jnp.dot(grad_q, wq.T, preferred_element_type=jnp.float32)
            + jnp.dot(grad_k, wk_tiled.T, preferred_element_type=jnp.float32)
            + jnp.dot(grad_v, wv_tiled.T, preferred_element_type=jnp.float32),
            rows_dev,
        )
        grad_in_norm, grad_gain_one = rms_back(layer_in, gain_pair[0], grad_normed_one)
        cotangent = grad_middle + grad_in_norm
        zero_heads = jnp.zeros((D, KV * HD), jnp.float32)
        grad_key = lax.dynamic_update_slice_in_dim(zero_heads, key_local, kv_head * HD, 1)
        grad_value = lax.dynamic_update_slice_in_dim(zero_heads, value_local, kv_head * HD, 1)
        grad_gain_pair = jnp.stack([grad_gain_one, grad_gain_two])
        large_grads = tuple(
            (
                lax.psum_scatter(
                    grad_query.astype(jnp.bfloat16), "dp", scatter_dimension=0, tiled=True
                ).astype(jnp.float32),
                lax.psum_scatter(
                    grad_out.astype(jnp.bfloat16), "dp", scatter_dimension=1, tiled=True
                ).astype(jnp.float32),
                lax.psum_scatter(
                    grad_gate.astype(jnp.bfloat16), "dp", scatter_dimension=0, tiled=True
                ).astype(jnp.float32),
                lax.psum_scatter(
                    grad_up.astype(jnp.bfloat16), "dp", scatter_dimension=0, tiled=True
                ).astype(jnp.float32),
                lax.psum_scatter(
                    grad_down.astype(jnp.bfloat16), "dp", scatter_dimension=1, tiled=True
                ).astype(jnp.float32),
            )
        )
        small_grads = tuple(
            (
                lax.psum_scatter(grad_key, ("dp", "tensor"), scatter_dimension=0, tiled=True),
                lax.psum_scatter(grad_value, ("dp", "tensor"), scatter_dimension=0, tiled=True),
                lax.psum_scatter(grad_gain_pair, ("dp", "tensor"), scatter_dimension=1, tiled=True),
            )
        )
        layer_grads[layer_index] = large_grads + small_grads
    stacked = [jnp.stack([layer_grads[0][kind]]) for kind in range(8)]
    return (
        output,
        cotangent,
        stacked[7],
        stacked[0],
        stacked[5],
        stacked[6],
        stacked[1],
        stacked[2],
        stacked[3],
        stacked[4],
    )


def solution(mesh):
    placed = (
        P(("dp", "tensor"), None),
        P("dp"),
        P(None, None, ("dp", "tensor")),
        P(None, "dp", "tensor"),
        P(None, ("dp", "tensor"), None),
        P(None, ("dp", "tensor"), None),
        P(None, "tensor", "dp"),
        P(None, "dp", "tensor"),
        P(None, "dp", "tensor"),
        P(None, "tensor", "dp"),
        P(("dp", "tensor"), None),
    )
    return jax.shard_map(
        on_device,
        mesh=mesh,
        in_specs=placed,
        out_specs=(
            P(("dp", "tensor"), None),
            P(("dp", "tensor"), None),
            P(None, None, ("dp", "tensor")),
            P(None, "dp", "tensor"),
            P(None, ("dp", "tensor"), None),
            P(None, ("dp", "tensor"), None),
            P(None, "tensor", "dp"),
            P(None, "dp", "tensor"),
            P(None, "dp", "tensor"),
            P(None, "tensor", "dp"),
        ),
        check_vma=False,
    )
```

profile of v0, /device:TPU:0, one launch (start us, length us, event | category | flops | bytes accessed | tf_op | source)
XLA Modules:
  0.0 2196.6 jit_solution(15463837602519331557)
XLA Ops:
  9.5 79.8 %all-gather = bf16[1,2,2048]{1,0,2:T(2,128)(2,1)S(1)} all-gather(bf16[1,2,64]{1,0,2:T(2,128)(2,1)S(1)} %copy.87), channel_id=2, replica_groups=mesh['dp'=8,'tensor'=4] {'dp','tensor'}, dimensions={2}, use_global_device_ids=true | all-gather | bytes 8448 | tf_op jit(solution)/shard_map/all_gather | solution.py:144
  91.7 33.5 %fusion.68 = (f32[2048]{0:T(1024)S(1)}, f32[2048]{0:T(1024)S(1)}) fusion(bf16[1,2,2048]{1,0,2:T(2,128)(2,1)S(1)} %all-gather), kind=kLoop, calls=%fused_computation.104 | loop fusion | flops 4096 | bytes 24576 | tf_op jit(solution)/shard_map/mul | solution.py:17
  131.0 75.3 %all-gather.20.cloned.1.call-done = bf16[1024,2048]{1,0:T(8,128)(2,1)} async-done(((bf16[256,2048]{1,0:T(8,128)(2,1)}), bf16[1024,2048]{1,0:T(8,128)(2,1)}) %all-gather.20.cloned.1.call-update) | async-done | bytes 4194320 | tf_op jit(solution)/shard_map/all_gather | solution.py:150
  213.4 20.9 all-gather.28.cloned.1.call-done
  240.5 49.7 %while.30 = (s32[]{:T(128)}, bf16[8,128,512]{2,1,0:T(8,128)(2,1)}, f32[8,1024]{1,0:T(8,128)}, bf16[8,128,512]{1,2,0:T(8,128)(2,1)S(1)}, bf16[8,128,64]{1,0,2:T(8...) while((s32[]{:T(128)}, bf16[8,128,512]{2,1,0:T(8,128)(2,1)}, f32[8,1024]{1,0:T(8,128)}, ...), condition=%wide.region_4.5_spmd, body=%wide.region_1.4_spmd.sunk | while | flops 34804736 | bytes 3300449 | solution.py:206
  302.1 140.4 %reduce-scatter.15.cloned.1.call-done = f32[256,2048]{1,0:T(8,128)} async-done(((f32[1024,2048]{1,0:T(8,128)}), f32[256,2048]{1,0:T(8,128)}) %reduce-scatter.15.cloned.1.call-update) | async-done | bytes 2097168 | tf_op jit(solution)/shard_map/reduce_scatter | solution.py:154
  447.9 78.1 %all-gather.24.cloned.1.call-done = bf16[1024,2048]{1,0:T(8,128)(2,1)} async-done(((bf16[256,2048]{1,0:T(8,128)(2,1)}), bf16[1024,2048]{1,0:T(8,128)(2,1)}) %all-gather.24.cloned.1.call-update) | async-done | bytes 4194320 | tf_op jit(solution)/shard_map/all_gather | solution.py:150
  526.0 44.7 %all-gather.40.cloned.1.call-done = bf16[1,1408,2048]{2,1,0:T(8,128)(2,1)} async-done(((bf16[1,1408,256]{2,1,0:T(8,128)(2,1)}), bf16[1,1408,2048]{2,1,0:T(8,128)(2,1)}) %all-gather.40.cloned.1.call-update) | async-done | bytes 5767184 | tf_op jit(solution)/shard_map/all_gather | solution.py:139
  582.4 33.4 %all-gather.38.cloned.1.call-done = bf16[1,2048,1408]{2,1,0:T(8,128)(2,1)} async-done(((bf16[1,256,1408]{2,1,0:T(8,128)(2,1)}), bf16[1,2048,1408]{2,1,0:T(8,128)(2,1)}) %all-gather.38.cloned.1.call-update) | async-done | bytes 5767184 | tf_op jit(solution)/shard_map/all_gather | solution.py:138
  615.8 82.8 %all-gather.22.cloned.1.call-done = bf16[1024,2048]{1,0:T(8,128)(2,1)} async-done(((bf16[256,2048]{1,0:T(8,128)(2,1)}), bf16[1024,2048]{1,0:T(8,128)(2,1)}) %all-gather.22.cloned.1.call-update) | async-done | bytes 4194320 | tf_op jit(solution)/shard_map/all_gather | solution.py:150
  710.2 31.9 %all-gather.36.cloned.1.call-done = bf16[1,2048,1408]{2,1,0:T(8,128)(2,1)} async-done(((bf16[1,256,1408]{2,1,0:T(8,128)(2,1)}), bf16[1,2048,1408]{2,1,0:T(8,128)(2,1)}) %all-gather.36.cloned.1.call-update) | async-done | bytes 5767184 | tf_op jit(solution)/shard_map/all_gather | solution.py:137
  790.4 132.6 %reduce-scatter.19.cloned.1.call-done = f32[256,2048]{1,0:T(8,128)} async-done(((f32[1024,2048]{1,0:T(8,128)}), f32[256,2048]{1,0:T(8,128)}) %reduce-scatter.19.cloned.1.call-update) | async-done | bytes 2097168 | tf_op jit(solution)/shard_map/reduce_scatter | solution.py:154
  925.8 144.9 %reduce-scatter.17.cloned.1.call-done = f32[256,2048]{1,0:T(8,128)} async-done(((f32[1024,2048]{1,0:T(8,128)}), f32[256,2048]{1,0:T(8,128)}) %reduce-scatter.17.cloned.1.call-update) | async-done | bytes 2097168 | tf_op jit(solution)/shard_map/reduce_scatter | solution.py:154
  1081.3 76.8 %all-gather.26.cloned.1.call-done = bf16[1024,2048]{1,0:T(8,128)(2,1)} async-done(((bf16[256,2048]{1,0:T(8,128)(2,1)}), bf16[1024,2048]{1,0:T(8,128)(2,1)}) %all-gather.26.cloned.1.call-update) | async-done | bytes 4194320 | tf_op jit(solution)/shard_map/all_gather | solution.py:150
  1163.4 171.1 %while.31 = (s32[]{:T(128)}, f32[8,128,512]{1,0,2:T(8,128)}, f32[8,128,512]{1,0,2:T(8,128)}, bf16[8,128,512]{2,1,0:T(8,128)(2,1)}, bf16[8,128,512]{1,2,0:T(8,128...) while((s32[]{:T(128)}, f32[8,128,512]{1,0,2:T(8,128)}, ...), condition=%wide.region_12.13_spmd, body=%wide.region_10.12_spmd.sunk | while | flops 85464064 | bytes 7626373 | solution.py:281
  1396.6 98.0 %reduce-scatter.21.cloned.1.call-done = f32[256,2048]{1,0:T(8,128)} async-done(((f32[1024,2048]{1,0:T(8,128)}), f32[256,2048]{1,0:T(8,128)}) %reduce-scatter.21.cloned.1.call-update) | async-done | bytes 2097168 | tf_op jit(solution)/shard_map/reduce_scatter | solution.py:154
  1528.2 29.4 %reduce-scatter.33.cloned.1.call-done = bf16[256,1408]{1,0:T(8,128)(2,1)} async-done(((bf16[2048,1408]{1,0:T(8,128)(2,1)}), bf16[256,1408]{1,0:T(8,128)(2,1)}) %reduce-scatter.33.cloned.1.call-update) | async-done | bytes 720912 | tf_op jit(solution)/shard_map/reduce_scatter | solution.py:326
  1559.8 60.0 %reduce-scatter.31.cloned.1.call-done = bf16[256,1408]{1,0:T(8,128)(2,1)} async-done(((bf16[2048,1408]{1,0:T(8,128)(2,1)}), bf16[256,1408]{1,0:T(8,128)(2,1)}) %reduce-scatter.31.cloned.1.call-update) | async-done | bytes 720912 | tf_op jit(solution)/shard_map/reduce_scatter | solution.py:323
  1622.2 59.9 %reduce-scatter.35.cloned.1.call-done = bf16[1408,256]{1,0:T(8,128)(2,1)} async-done(((bf16[1408,2048]{1,0:T(8,128)(2,1)}), bf16[1408,256]{1,0:T(8,128)(2,1)}) %reduce-scatter.35.cloned.1.call-update) | async-done | bytes 720912 | tf_op jit(solution)/shard_map/reduce_scatter | solution.py:329
  1684.4 42.1 %reduce-scatter.23.cloned.1.call-done = bf16[256,512]{1,0:T(8,128)(2,1)} async-done(((bf16[2048,512]{1,0:T(8,128)(2,1)}), bf16[256,512]{1,0:T(8,128)(2,1)}) %reduce-scatter.23.cloned.1.call-update) | async-done | bytes 262160 | tf_op jit(solution)/shard_map/reduce_scatter | solution.py:317
  1728.3 42.5 %reduce-scatter.29.cloned.1.call-done = bf16[512,256]{1,0:T(8,128)(2,1)} async-done(((bf16[512,2048]{1,0:T(8,128)(2,1)}), bf16[512,256]{1,0:T(8,128)(2,1)}) %reduce-scatter.29.cloned.1.call-update) | async-done | bytes 262160 | tf_op jit(solution)/shard_map/reduce_scatter | solution.py:320
  1776.6 133.5 %reduce-scatter.37.cloned.1.call-done = f32[64,2]{1,0:T(8,128)} async-done(((f32[2048,2]{1,0:T(8,128)}), f32[64,2]{1,0:T(8,128)}) %reduce-scatter.37.cloned.1.call-update) | async-done | bytes 528
  1911.5 138.2 %reduce-scatter.25.cloned.1.call-done = f32[64,256]{1,0:T(8,128)} async-done(((f32[2048,256]{1,0:T(8,128)}), f32[64,256]{1,0:T(8,128)}) %reduce-scatter.25.cloned.1.call-update) | async-done | bytes 65552 | tf_op jit(solution)/shard_map/reduce_scatter | solution.py:336
  2049.7 140.2 %reduce-scatter.27.cloned.1.call-done = f32[64,256]{1,0:T(8,128)} async-done(((f32[2048,256]{1,0:T(8,128)}), f32[64,256]{1,0:T(8,128)}) %reduce-scatter.27.cloned.1.call-update) | async-done | bytes 65552 | tf_op jit(solution)/shard_map/reduce_scatter | solution.py:337
  (432 shorter events, 462.0 us)
Async XLA Ops:
  7.2 122.2 %all-gather.30.cloned.1.call-start = ((), (), s32[]{:S(2)}) async-start(), calls=%async_computation.28 | async-start | bytes 1081344 | tf_op jit(solution)/shard_map/all_gather | solution.py:142
  7.9 121.5 %all-gather.32.cloned.1.call-start = ((), (), s32[]{:S(2)}) async-start(), calls=%async_computation.29 | async-start | bytes 1081344 | tf_op jit(solution)/shard_map/all_gather | solution.py:143
  8.7 197.6 %all-gather.20.cloned.1.call-start = ((), (), s32[]{:S(2)}) async-start(), calls=%async_computation.12 | async-start | bytes 5242880 | tf_op jit(solution)/shard_map/all_gather | solution.py:150
  127.0 107.3 %all-gather.28.cloned.1.call-start = ((), (), s32[]{:S(2)}) async-start(), calls=%async_computation.27 | async-start | bytes 2359296 | tf_op jit(solution)/shard_map/all_gather | solution.py:135
  127.6 162.6 %all-gather.34.cloned.1.call-start = ((), (), s32[]{:S(2)}) async-start(), calls=%async_computation.30 | async-start | bytes 2359296 | tf_op jit(solution)/shard_map/all_gather | solution.py:136
  128.2 314.3 %reduce-scatter.15.cloned.1.call-start = ((), (), s32[]{:S(2)}) async-start(), calls=%async_computation.13 | async-start | bytes 10485760 | tf_op jit(solution)/shard_map/reduce_scatter | solution.py:154
  297.8 228.3 %all-gather.24.cloned.1.call-start = ((), (), s32[]{:S(2)}) async-start(), calls=%async_computation.16 | async-start | bytes 5242880 | tf_op jit(solution)/shard_map/all_gather | solution.py:150
  300.5 270.2 %all-gather.40.cloned.1.call-start = ((), (), s32[]{:S(2)}) async-start(), calls=%async_computation.33 | async-start | bytes 6488064 | tf_op jit(solution)/shard_map/all_gather | solution.py:139
  301.3 314.5 %all-gather.38.cloned.1.call-start = ((), (), s32[]{:S(2)}) async-start(), calls=%async_computation.32 | async-start | bytes 6488064 | tf_op jit(solution)/shard_map/all_gather | solution.py:138
  302.0 396.5 %all-gather.22.cloned.1.call-start = ((), (), s32[]{:S(2)}) async-start(), calls=%async_computation.14 | async-start | bytes 5242880 | tf_op jit(solution)/shard_map/all_gather | solution.py:150
  447.0 295.2 %all-gather.36.cloned.1.call-start = ((), (), s32[]{:S(2)}) async-start(), calls=%async_computation.31 | async-start | bytes 6488064 | tf_op jit(solution)/shard_map/all_gather | solution.py:137
  447.7 475.3 %reduce-scatter.19.cloned.1.call-start = ((), (), s32[]{:S(2)}) async-start(), calls=%async_computation.17 | async-start | bytes 10485760 | tf_op jit(solution)/shard_map/reduce_scatter | solution.py:154
  778.3 292.4 %reduce-scatter.17.cloned.1.call-start = ((), (), s32[]{:S(2)}) async-start(), calls=%async_computation.15 | async-start | bytes 10485760 | tf_op jit(solution)/shard_map/reduce_scatter | solution.py:154
  790.4 367.7 %all-gather.26.cloned.1.call-start = ((), (), s32[]{:S(2)}) async-start(), calls=%async_computation.18 | async-start | bytes 5242880 | tf_op jit(solution)/shard_map/all_gather | solution.py:150
  1076.6 417.9 %reduce-scatter.21.cloned.1.call-start = ((), (), s32[]{:S(2)}) async-start(), calls=%async_computation.19 | async-start | bytes 10485760 | tf_op jit(solution)/shard_map/reduce_scatter | solution.py:154
  1351.3 206.3 %reduce-scatter.33.cloned.1.call-start = ((), (), s32[]{:S(2)}) async-start(), calls=%async_computation.25 | async-start | bytes 6488064 | tf_op jit(solution)/shard_map/reduce_scatter | solution.py:326
  1362.5 257.3 %reduce-scatter.31.cloned.1.call-start = ((), (), s32[]{:S(2)}) async-start(), calls=%async_computation.24 | async-start | bytes 6488064 | tf_op jit(solution)/shard_map/reduce_scatter | solution.py:323
  1373.6 308.4 %reduce-scatter.35.cloned.1.call-start = ((), (), s32[]{:S(2)}) async-start(), calls=%async_computation.26 | async-start | bytes 6488064 | tf_op jit(solution)/shard_map/reduce_scatter | solution.py:329
  1384.2 342.3 %reduce-scatter.23.cloned.1.call-start = ((), (), s32[]{:S(2)}) async-start(), calls=%async_computation.20 | async-start | bytes 2359296 | tf_op jit(solution)/shard_map/reduce_scatter | solution.py:317
  1390.3 380.5 %reduce-scatter.29.cloned.1.call-start = ((), (), s32[]{:S(2)}) async-start(), calls=%async_computation.23 | async-start | bytes 2359296 | tf_op jit(solution)/shard_map/reduce_scatter | solution.py:320
  1396.5 513.6 %reduce-scatter.37.cloned.1.call-start = ((), (), s32[]{:S(2)}) async-start(), calls=%async_computation.34 | async-start | bytes 1081344
  1498.1 551.6 %reduce-scatter.25.cloned.1.call-start = ((), (), s32[]{:S(2)}) async-start(), calls=%async_computation.21 | async-start | bytes 2162688 | tf_op jit(solution)/shard_map/reduce_scatter | solution.py:336
  1512.4 677.5 %reduce-scatter.27.cloned.1.call-start = ((), (), s32[]{:S(2)}) async-start(), calls=%async_computation.22 | async-start | bytes 2162688 | tf_op jit(solution)/shard_map/reduce_scatter | solution.py:337
  1559.8 212.7 %copy-start.21 = (f32[256]{0:T(256)S(1)}, f32[256]{0:T(256)}, u32[]{:S(2)}) copy-start(f32[256]{0:T(256)} %get-tuple-element.349) | copy-start | bytes 3076
  (28 other events, 1076.8 us)
Sparse Core Ops, SparseCore 0:
  11.0 57.2 all-gather.29
  71.3 53.0 all-gather.31
  127.1 79.0 all-gather.19
  208.0 26.2 all-gather.27
  236.0 28.0 all-gather.33
  297.9 144.6 reduce-scatter.14
  444.7 81.3 all-gather.23
  527.9 42.7 all-gather.39
  572.6 43.1 all-gather.37
  617.8 80.7 all-gather.21
  700.5 41.6 all-gather.35
  778.4 144.6 reduce-scatter.18
  925.4 145.2 reduce-scatter.16
  1076.7 81.3 all-gather.25
  1351.4 143.0 reduce-scatter.20
  1497.8 59.6 reduce-scatter.32
  1560.8 58.9 reduce-scatter.30
  1623.2 58.8 reduce-scatter.34
  1685.3 41.1 reduce-scatter.22
  1729.6 41.1 reduce-scatter.28
  1773.0 137.0 reduce-scatter.36
  1913.0 136.6 reduce-scatter.24
  2052.5 137.3 reduce-scatter.26
where the time goes:
time: 2210 us; the launch traced here: 2200 us
  waiting for transfers between devices  1610 us (73%)
  local copies, waits for them, and re-layouts  207 us (9%)
  matrix products  204 us (9%)
  blocking collectives  79.8 us (4%)
  other arithmetic  78.1 us (4%)
    reduce_scatter x4, waiting for transfers between devices, sum_rows(): lax.psum_scatter(term(jnp.int32(0), rows_dev * lax.axis_size('tensor')),...  516 us
    all_gather x4, waiting for transfers between devices, gather_rows(): return lax.all_gather(row_vals, 'tensor', axis=0, tiled=True)  313 us
    reduce_scatter x1, waiting for transfers between devices, on_device(): lax.psum_scatter(grad_value, ('dp', 'tensor'), scatter_dimension=0, tiled...  140 us
    unnamed x24, waiting for transfers between devices  138 us
    reduce_scatter x1, waiting for transfers between devices, on_device(): lax.psum_scatter(grad_key, ('dp', 'tensor'), scatter_dimension=0, tiled=T...  138 us
    dynamic_update_slice x32, local copies, waits for them, and re-layouts, on_device(): lax.map(one_backward, (by_sequence(query_all), by_sequence(key_all), by_s...  135 us
    all_gather x1, blocking collectives, fetch_weights(): lax.all_gather(norm_gains[layer_index], ('dp', 'tensor'), axis=1, tiled=T...  79.8 us
    reduce_scatter x1, waiting for transfers between devices, on_device(): lax.psum_scatter(grad_gate.astype(jnp.bfloat16), 'dp', scatter_dimension=...  60 us
  transfers between devices with their start and end apart: 23, of which 20 were waited for; matrix products, arithmetic and copies ran while one was open for 11% of the time, Pallas kernels for 0%

commit v1 on v0

--- a/solution.py
+++ b/solution.py
@@ -147,7 +147,31 @@
 
 
 def gather_rows(row_vals):
-    return lax.all_gather(row_vals, "tensor", axis=0, tiled=True)
+
+    def push_domain(load):
+        a_name = "tensor"
+        b_next = jax.lax.psum(1, axis_name=a_name)
+        f_next = jax.lax.axis_index(a_name)
+        before, moved, a_next = (b_next, f_next, load.shape[0])
+        blocks_here = [(num, (num + 1) % before) for num in range(before)]
+        views = [(num, (num - 1) % before) for num in range(before)]
+        response = jnp.zeros((*load.shape[:0], before * a_next, *load.shape[1:]), load.dtype)
+        response = lax.dynamic_update_slice_in_dim(response, load, moved * a_next, axis=0)
+        value_now = before // 2
+        v_next = extra = load
+        for j0 in range(1, value_now + 1):
+            v_next = jax.lax.ppermute(v_next, axis_name=a_name, perm=blocks_here)
+            response = lax.dynamic_update_slice_in_dim(
+                response, v_next, (moved - j0) % before * a_next, axis=0
+            )
+            if j0 < before - value_now:
+                extra = jax.lax.ppermute(extra, perm=views, axis_name=a_name)
+                response = lax.dynamic_update_slice_in_dim(
+                    response, extra, (moved + j0) % before * a_next, axis=0
+                )
+        return response
+
+    return push_domain(row_vals)
 
 
 def sum_rows(term, rows_dev):

time: 2210 us -> 2080 us (0.941)
  waiting for transfers between devices: 1610 us -> 1360 us
  starting transfers between devices: 2.19 us -> 85.5 us
  local copies, waits for them, and re-layouts: 207 us -> 242 us
    all_gather x4 -> x0, waiting for transfers between devices: 313 us -> none  [gather_rows(): return lax.all_gather(row_vals, 'tensor', axis=0, tiled=True)]
    ppermute x0 -> x12, waiting for transfers between devices: none -> 166 us  [the longest x8 150 us: push_domain(): v_next = jax.lax.ppermute(v_next, axis_name=a_name, perm=blocks_here)]
    ppermute x0 -> x12, starting transfers between devices: none -> 84.5 us  [the longest x8 70.2 us: push_domain(): v_next = jax.lax.ppermute(v_next, axis_name=a_name, perm=blocks_here)]
    all_gather x1, waiting for transfers between devices: 44.7 us -> 0.01 us  [fetch_weights(): lax.all_gather(w_down[layer_index], 'dp', axis=1, tiled=True)]
    dynamic_update_slice x0 -> x12, local copies, waits for them, and re-layouts: none -> 24.3 us  [the longest x8 14.9 us: push_domain(): lax.dynamic_update_slice_in_dim(response, v_next, (moved - j0) % before *...]
    unnamed x24 -> x20, waiting for transfers between devices: 138 us -> 137 us
  transfers between devices with their start and end apart: 23 -> 31, of which waited for: 20 -> 22; matrix products, arithmetic and copies ran while one was open for 11% -> 13% of each run, Pallas kernels for 0% -> 0%
where the time goes in v1:
time: 2080 us; the launch traced here: 2070 us
  waiting for transfers between devices  1360 us (65%)
  local copies, waits for them, and re-layouts  242 us (12%)
  matrix products  205 us (10%)
  starting transfers between devices  85.5 us (4%)
  blocking collectives  79.8 us (4%)
  other arithmetic  76 us (4%)
    reduce_scatter x4, waiting for transfers between devices, sum_rows(): lax.psum_scatter(term(jnp.int32(0), rows_dev * lax.axis_size('tensor')),...  499 us
    ppermute x8, waiting for transfers between devices, push_domain(): v_next = jax.lax.ppermute(v_next, axis_name=a_name, perm=blocks_here)  150 us
    reduce_scatter x1, waiting for transfers between devices, on_device(): lax.psum_scatter(grad_key, ('dp', 'tensor'), scatter_dimension=0, tiled=T...  140 us
    reduce_scatter x1, waiting for transfers between devices, on_device(): lax.psum_scatter(grad_value, ('dp', 'tensor'), scatter_dimension=0, tiled...  138 us
    unnamed x20, waiting for transfers between devices  137 us
    dynamic_update_slice x32, local copies, waits for them, and re-layouts, on_device(): lax.map(one_backward, (by_sequence(query_all), by_sequence(key_all), by_s...  135 us
    all_gather x1, blocking collectives, fetch_weights(): lax.all_gather(norm_gains[layer_index], ('dp', 'tensor'), axis=1, tiled=T...  79.8 us
    ppermute x8, starting transfers between devices, push_domain(): v_next = jax.lax.ppermute(v_next, axis_name=a_name, perm=blocks_here)  70.2 us
  transfers between devices with their start and end apart: 31, of which 22 were waited for; matrix products, arithmetic and copies ran while one was open for 13% of the time, Pallas kernels for 0%

profile of v1, /device:TPU:0, one launch (start us, length us, event | category | flops | bytes accessed | tf_op | source)
XLA Modules:
  0.0 2069.1 jit_solution(12077392701916140325)
XLA Ops:
  10.2 79.8 %all-gather = bf16[1,2,2048]{1,0,2:T(2,128)(2,1)S(1)} all-gather(bf16[1,2,64]{1,0,2:T(2,128)(2,1)S(1)} %copy.87), channel_id=2, replica_groups=mesh['dp'=8,'tensor'=4] {'dp','tensor'}, dimensions={2}, use_global_device_ids=true | all-gather | bytes 8448 | tf_op jit(solution)/shard_map/all_gather | solution.py:144
  92.6 33.9 %fusion.68 = (f32[2048]{0:T(1024)S(1)}, f32[2048]{0:T(1024)S(1)}) fusion(bf16[1,2,2048]{1,0,2:T(2,128)(2,1)S(1)} %all-gather), kind=kLoop, calls=%fused_computation.104 | loop fusion | flops 4096 | bytes 24576 | tf_op jit(solution)/shard_map/mul | solution.py:17
  134.4 23.9 %collective-permute-done = bf16[256,2048]{1,0:T(8,128)(2,1)} collective-permute-done((bf16[256,2048]{1,0:T(8,128)(2,1)S(1)}, bf16[256,2048]{1,0:T(8,128)(2,1)}, u32[]{:S(2)}, u32[]{:S(2)}) %collective-permute-start) | collective-permute-done | bytes 1048608 | tf_op jit(solution)/shard_map/ppermute | solution.py:163
  214.7 49.7 %while.30 = (s32[]{:T(128)}, bf16[8,128,512]{2,1,0:T(8,128)(2,1)}, f32[8,1024]{1,0:T(8,128)}, bf16[8,128,512]{1,2,0:T(8,128)(2,1)S(1)}, bf16[8,128,64]{1,0,2:T(8...) while((s32[]{:T(128)}, bf16[8,128,512]{2,1,0:T(8,128)(2,1)}, f32[8,1024]{1,0:T(8,128)}, ...), condition=%wide.region_4.5_spmd, body=%wide.region_1.4_spmd.sunk | while | flops 34804736 | bytes 3300449 | solution.py:230
  282.4 46.8 %collective-permute-done.6 = bf16[256,2048]{1,0:T(8,128)(2,1)} collective-permute-done((bf16[256,2048]{1,0:T(8,128)(2,1)}, bf16[256,2048]{1,0:T(8,128)(2,1)}, u32[]{:S(2)}, u32[]{:S(2)}) %collective-permute-start.6) | collective-permute-done | bytes 1048608 | tf_op jit(solution)/shard_map/ppermute | solution.py:163
  329.2 27.0 %collective-permute-start.8 = (bf16[256,2048]{1,0:T(8,128)(2,1)}, bf16[256,2048]{1,0:T(8,128)(2,1)}, u32[]{:S(2)}, u32[]{:S(2)}) collective-permute-start(bf16[256,2048]{1,0:T(8,128)(2,1)} %collective-permute-done.6), channel_id=1, source_target_pairs={{0,1},{1,2},{2,3},{3,0},{4,5},{5,6},{6,7},{7,4},{8,9},{9,10},{10,1... | collective-permute-start | bytes 3145736 | tf_op jit(solution)/shard_map/ppermute | solution.py:163
  356.1 122.7 %reduce-scatter.15.cloned.1.call-done = f32[256,2048]{1,0:T(8,128)} async-done(((f32[1024,2048]{1,0:T(8,128)}), f32[256,2048]{1,0:T(8,128)}) %reduce-scatter.15.cloned.1.call-update) | async-done | bytes 2097168 | tf_op jit(solution)/shard_map/reduce_scatter | solution.py:178
  495.7 16.9 collective-permute-done.3
  512.6 20.6 collective-permute-start.5
  584.9 33.4 %all-gather.24.cloned.1.call-done = bf16[1,2048,1408]{2,1,0:T(8,128)(2,1)} async-done(((bf16[1,256,1408]{2,1,0:T(8,128)(2,1)}), bf16[1,2048,1408]{2,1,0:T(8,128)(2,1)}) %all-gather.24.cloned.1.call-update) | async-done | bytes 5767184 | tf_op jit(solution)/shard_map/all_gather | solution.py:137
  666.4 133.0 %reduce-scatter.19.cloned.1.call-done = f32[256,2048]{1,0:T(8,128)} async-done(((f32[1024,2048]{1,0:T(8,128)}), f32[256,2048]{1,0:T(8,128)}) %reduce-scatter.19.cloned.1.call-update) | async-done | bytes 2097168 | tf_op jit(solution)/shard_map/reduce_scatter | solution.py:178
  799.4 147.5 %reduce-scatter.17.cloned.1.call-done = f32[256,2048]{1,0:T(8,128)} async-done(((f32[1024,2048]{1,0:T(8,128)}), f32[256,2048]{1,0:T(8,128)}) %reduce-scatter.17.cloned.1.call-update) | async-done | bytes 2097168 | tf_op jit(solution)/shard_map/reduce_scatter | solution.py:178
  962.0 24.3 %collective-permute-done.9 = bf16[256,2048]{1,0:T(8,128)(2,1)S(1)} collective-permute-done((bf16[256,2048]{1,0:T(8,128)(2,1)}, bf16[256,2048]{1,0:T(8,128)(2,1)S(1)}, u32[]{:S(2)}, u32[]{:S(2)}) %collective-permute-start.9) | collective-permute-done | bytes 1048608 | tf_op jit(solution)/shard_map/ppermute | solution.py:163
  986.2 21.6 %collective-permute-start.11 = (bf16[256,2048]{1,0:T(8,128)(2,1)S(1)}, bf16[256,2048]{1,0:T(8,128)(2,1)S(1)}, u32[]{:S(2)}, u32[]{:S(2)}) collective-permute-start(bf16[256,2048]{1,0:T(8,128)(2,1)S(1)} %collective-permute-done.9), channel_id=1, source_target_pairs={{0,1},{1,2},{2,3},{3,0},{4,5},{5,6},{6,7},{7,4},{8,9},{9,10},{10,1... | collective-permute-start | bytes 3145736 | tf_op jit(solution)/shard_map/ppermute | solution.py:163
  1035.3 171.4 %while.31 = (s32[]{:T(128)}, f32[8,128,512]{1,0,2:T(8,128)}, f32[8,128,512]{1,0,2:T(8,128)}, bf16[8,128,512]{2,1,0:T(8,128)(2,1)}, bf16[8,128,512]{1,2,0:T(8,128...) while((s32[]{:T(128)}, f32[8,128,512]{1,0,2:T(8,128)}, ...), condition=%wide.region_12.13_spmd, body=%wide.region_10.12_spmd.sunk | while | flops 85464064 | bytes 7626373 | solution.py:305
  1270.9 96.2 %reduce-scatter.21.cloned.1.call-done = f32[256,2048]{1,0:T(8,128)} async-done(((f32[1024,2048]{1,0:T(8,128)}), f32[256,2048]{1,0:T(8,128)}) %reduce-scatter.21.cloned.1.call-update) | async-done | bytes 2097168 | tf_op jit(solution)/shard_map/reduce_scatter | solution.py:178
  1399.7 30.3 %reduce-scatter.33.cloned.1.call-done = bf16[256,1408]{1,0:T(8,128)(2,1)} async-done(((bf16[2048,1408]{1,0:T(8,128)(2,1)}), bf16[256,1408]{1,0:T(8,128)(2,1)}) %reduce-scatter.33.cloned.1.call-update) | async-done | bytes 720912 | tf_op jit(solution)/shard_map/reduce_scatter | solution.py:350
  1432.4 60.2 %reduce-scatter.31.cloned.1.call-done = bf16[256,1408]{1,0:T(8,128)(2,1)} async-done(((bf16[2048,1408]{1,0:T(8,128)(2,1)}), bf16[256,1408]{1,0:T(8,128)(2,1)}) %reduce-scatter.31.cloned.1.call-update) | async-done | bytes 720912 | tf_op jit(solution)/shard_map/reduce_scatter | solution.py:347
  1494.9 59.9 %reduce-scatter.35.cloned.1.call-done = bf16[1408,256]{1,0:T(8,128)(2,1)} async-done(((bf16[1408,2048]{1,0:T(8,128)(2,1)}), bf16[1408,256]{1,0:T(8,128)(2,1)}) %reduce-scatter.35.cloned.1.call-update) | async-done | bytes 720912 | tf_op jit(solution)/shard_map/reduce_scatter | solution.py:353
  1557.1 42.0 %reduce-scatter.29.cloned.1.call-done = bf16[512,256]{1,0:T(8,128)(2,1)} async-done(((bf16[512,2048]{1,0:T(8,128)(2,1)}), bf16[512,256]{1,0:T(8,128)(2,1)}) %reduce-scatter.29.cloned.1.call-update) | async-done | bytes 262160 | tf_op jit(solution)/shard_map/reduce_scatter | solution.py:344
  1600.8 42.5 %reduce-scatter.23.cloned.1.call-done = bf16[256,512]{1,0:T(8,128)(2,1)} async-done(((bf16[2048,512]{1,0:T(8,128)(2,1)}), bf16[256,512]{1,0:T(8,128)(2,1)}) %reduce-scatter.23.cloned.1.call-update) | async-done | bytes 262160 | tf_op jit(solution)/shard_map/reduce_scatter | solution.py:341
  1649.3 133.2 %reduce-scatter.37.cloned.1.call-done = f32[64,2]{1,0:T(8,128)} async-done(((f32[2048,2]{1,0:T(8,128)}), f32[64,2]{1,0:T(8,128)}) %reduce-scatter.37.cloned.1.call-update) | async-done | bytes 528
  1783.8 138.2 %reduce-scatter.27.cloned.1.call-done = f32[64,256]{1,0:T(8,128)} async-done(((f32[2048,256]{1,0:T(8,128)}), f32[64,256]{1,0:T(8,128)}) %reduce-scatter.27.cloned.1.call-update) | async-done | bytes 65552 | tf_op jit(solution)/shard_map/reduce_scatter | solution.py:361
  1922.0 140.3 %reduce-scatter.25.cloned.1.call-done = f32[64,256]{1,0:T(8,128)} async-done(((f32[2048,256]{1,0:T(8,128)}), f32[64,256]{1,0:T(8,128)}) %reduce-scatter.25.cloned.1.call-update) | async-done | bytes 65552 | tf_op jit(solution)/shard_map/reduce_scatter | solution.py:360
  (474 shorter events, 578.5 us)
Async XLA Ops:
  7.2 172.3 %all-gather.18.cloned.1.call-start = ((), (), s32[]{:S(2)}) async-start(), calls=%async_computation.24 | async-start | bytes 1081344 | tf_op jit(solution)/shard_map/all_gather | solution.py:142
  7.9 171.6 %all-gather.20.cloned.1.call-start = ((), (), s32[]{:S(2)}) async-start(), calls=%async_computation.25 | async-start | bytes 1081344 | tf_op jit(solution)/shard_map/all_gather | solution.py:143
  8.7 199.9 %all-gather.16.cloned.1.call-start = ((), (), s32[]{:S(2)}) async-start(), calls=%async_computation.23 | async-start | bytes 2359296 | tf_op jit(solution)/shard_map/all_gather | solution.py:135
  9.4 255.0 %all-gather.22.cloned.1.call-start = ((), (), s32[]{:S(2)}) async-start(), calls=%async_computation.26 | async-start | bytes 2359296 | tf_op jit(solution)/shard_map/all_gather | solution.py:136
  134.2 344.7 %reduce-scatter.15.cloned.1.call-start = ((), (), s32[]{:S(2)}) async-start(), calls=%async_computation.12 | async-start | bytes 10485760 | tf_op jit(solution)/shard_map/reduce_scatter | solution.py:178
  272.0 261.2 %all-gather.28.cloned.1.call-start = ((), (), s32[]{:S(2)}) async-start(), calls=%async_computation.29 | async-start | bytes 6488064 | tf_op jit(solution)/shard_map/all_gather | solution.py:139
  272.6 300.6 %all-gather.26.cloned.1.call-start = ((), (), s32[]{:S(2)}) async-start(), calls=%async_computation.28 | async-start | bytes 6488064 | tf_op jit(solution)/shard_map/all_gather | solution.py:138
  273.3 345.0 %all-gather.24.cloned.1.call-start = ((), (), s32[]{:S(2)}) async-start(), calls=%async_computation.27 | async-start | bytes 6488064 | tf_op jit(solution)/shard_map/all_gather | solution.py:137
  274.1 525.3 %reduce-scatter.19.cloned.1.call-start = ((), (), s32[]{:S(2)}) async-start(), calls=%async_computation.14 | async-start | bytes 10485760 | tf_op jit(solution)/shard_map/reduce_scatter | solution.py:178
  278.5 50.6 %collective-permute-start.6 = (bf16[256,2048]{1,0:T(8,128)(2,1)}, bf16[256,2048]{1,0:T(8,128)(2,1)}, u32[]{:S(2)}, u32[]{:S(2)}) collective-permute-start(bf16[256,2048]{1,0:T(8,128)(2,1)} %get-tuple-element.325), channel_id=1, source_target_pairs={{0,1},{1,2},{2,3},{3,0},{4,5},{5,6},{6,7},{7,4},{8,9},{9,10},{10,1... | collective-permute-start | bytes 3145736 | tf_op jit(solution)/shard_map/ppermute | solution.py:163
  278.6 208.5 %collective-permute-start.7 = (bf16[256,2048]{1,0:T(8,128)(2,1)}, bf16[256,2048]{1,0:T(8,128)(2,1)}, u32[]{:S(2)}, u32[]{:S(2)}) collective-permute-start(bf16[256,2048]{1,0:T(8,128)(2,1)} %get-tuple-element.325), channel_id=1, source_target_pairs={{0,3},{1,0},{2,1},{3,2},{4,7},{5,4},{6,5},{7,6},{8,11},{9,8},{10,9... | collective-permute-start | bytes 3145736 | tf_op jit(solution)/shard_map/ppermute | solution.py:168
  329.2 160.3 %collective-permute-start.8 = (bf16[256,2048]{1,0:T(8,128)(2,1)}, bf16[256,2048]{1,0:T(8,128)(2,1)}, u32[]{:S(2)}, u32[]{:S(2)}) collective-permute-start(bf16[256,2048]{1,0:T(8,128)(2,1)} %collective-permute-done.6), channel_id=1, source_target_pairs={{0,1},{1,2},{2,3},{3,0},{4,5},{5,6},{6,7},{7,4},{8,9},{9,10},{10,1... | collective-permute-start | bytes 3145736 | tf_op jit(solution)/shard_map/ppermute | solution.py:163
  491.9 54.2 %collective-permute-start.4 = (bf16[256,2048]{1,0:T(8,128)(2,1)S(1)}, bf16[256,2048]{1,0:T(8,128)(2,1)}, u32[]{:S(2)}, u32[]{:S(2)}) collective-permute-start(bf16[256,2048]{1,0:T(8,128)(2,1)S(1)} %get-tuple-element.327), channel_id=1, source_target_pairs={{0,3},{1,0},{2,1},{3,2},{4,7},{5,4},{6,5},{7,6},{8,11},{9,8},{10,9... | collective-permute-start | bytes 3145736 | tf_op jit(solution)/shard_map/ppermute | solution.py:168
  654.6 292.2 %reduce-scatter.17.cloned.1.call-start = ((), (), s32[]{:S(2)}) async-start(), calls=%async_computation.13 | async-start | bytes 10485760 | tf_op jit(solution)/shard_map/reduce_scatter | solution.py:178
  666.3 700.8 %reduce-scatter.21.cloned.1.call-start = ((), (), s32[]{:S(2)}) async-start(), calls=%async_computation.15 | async-start | bytes 10485760 | tf_op jit(solution)/shard_map/reduce_scatter | solution.py:178
  959.2 54.3 %collective-permute-start.10 = (bf16[256,2048]{1,0:T(8,128)(2,1)}, bf16[256,2048]{1,0:T(8,128)(2,1)}, u32[]{:S(2)}, u32[]{:S(2)}) collective-permute-start(bf16[256,2048]{1,0:T(8,128)(2,1)} %get-tuple-element.322), channel_id=1, source_target_pairs={{0,3},{1,0},{2,1},{3,2},{4,7},{5,4},{6,5},{7,6},{8,11},{9,8},{10,9... | collective-permute-start | bytes 3145736 | tf_op jit(solution)/shard_map/ppermute | solution.py:168
  1223.2 206.8 %reduce-scatter.33.cloned.1.call-start = ((), (), s32[]{:S(2)}) async-start(), calls=%async_computation.21 | async-start | bytes 6488064 | tf_op jit(solution)/shard_map/reduce_scatter | solution.py:350
  1234.5 258.1 %reduce-scatter.31.cloned.1.call-start = ((), (), s32[]{:S(2)}) async-start(), calls=%async_computation.20 | async-start | bytes 6488064 | tf_op jit(solution)/shard_map/reduce_scatter | solution.py:347
  1245.5 309.2 %reduce-scatter.35.cloned.1.call-start = ((), (), s32[]{:S(2)}) async-start(), calls=%async_computation.22 | async-start | bytes 6488064 | tf_op jit(solution)/shard_map/reduce_scatter | solution.py:353
  1256.1 343.0 %reduce-scatter.29.cloned.1.call-start = ((), (), s32[]{:S(2)}) async-start(), calls=%async_computation.19 | async-start | bytes 2359296 | tf_op jit(solution)/shard_map/reduce_scatter | solution.py:344
  1263.3 380.1 %reduce-scatter.23.cloned.1.call-start = ((), (), s32[]{:S(2)}) async-start(), calls=%async_computation.16 | async-start | bytes 2359296 | tf_op jit(solution)/shard_map/reduce_scatter | solution.py:341
  1269.5 512.9 %reduce-scatter.37.cloned.1.call-start = ((), (), s32[]{:S(2)}) async-start(), calls=%async_computation.30 | async-start | bytes 1081344
  1370.7 551.3 %reduce-scatter.27.cloned.1.call-start = ((), (), s32[]{:S(2)}) async-start(), calls=%async_computation.18 | async-start | bytes 2162688 | tf_op jit(solution)/shard_map/reduce_scatter | solution.py:361
  1385.1 677.2 %reduce-scatter.25.cloned.1.call-start = ((), (), s32[]{:S(2)}) async-start(), calls=%async_computation.17 | async-start | bytes 2162688 | tf_op jit(solution)/shard_map/reduce_scatter | solution.py:360
  (43 other events, 1697.8 us)
Sparse Core Ops, SparseCore 0:
  11.0 56.7 all-gather.17
  70.8 53.2 all-gather.19
  125.9 26.7 all-gather.15
  154.4 28.0 all-gather.21
  272.1 206.6 reduce-scatter.14
  480.6 47.4 all-gather.27
  530.0 43.1 all-gather.25
  575.1 43.1 all-gather.23
  654.7 144.6 reduce-scatter.18
  801.6 145.2 reduce-scatter.16
  1223.4 143.6 reduce-scatter.20
  1370.4 59.6 reduce-scatter.32
  1433.5 59.0 reduce-scatter.30
  1495.9 58.8 reduce-scatter.34
  1557.9 41.1 reduce-scatter.28
  1602.2 41.1 reduce-scatter.22
  1645.5 136.9 reduce-scatter.36
  1785.1 136.8 reduce-scatter.26
  1924.8 137.4 reduce-scatter.24
